TPU v7x, 32 devices: a whole 2x2x4 slice. The times are simulated.
32 devices in a mesh: outer: 2 (over y), inner: 4 (over x, core), heads: 4 (over z).
Axes of the slice: x: 2, y: 2, z: 4, core: 2. Of those that a mesh axis runs over, the one named last changes fastest.
Arguments:
- raw_keys: bfloat16 [8, 4096, 8, 128], P(None, ('outer', 'inner'), 'heads'), may hold values from -6 to 6
- raw_values: bfloat16 [8, 4096, 8, 128], P(None, ('outer', 'inner'), 'heads'), may hold values from -6 to 6
- turn_angle: float32 [4096, 64], replicated, may hold values from -3.140625 to 3.140625
Outputs:
- stored_keys: bfloat16 [8, 4096, 8, 128], P(('outer', 'inner'), None, 'heads')
- stored_values: bfloat16 [8, 4096, 8, 128], P(('outer', 'inner'), None, 'heads')
- page_high: bfloat16 [8, 64, 8, 128], P(('outer', 'inner'), None, 'heads')
- page_low: bfloat16 [8, 64, 8, 128], P(('outer', 'inner'), None, 'heads')
All inputs are finite; a program needn't handle non-finite values.
Results may differ from a plain program's by a relative error of at most 0.001.
Values may be sent and summed in bfloat16 or wider, within the bound.
A program may use at most 128 MiB of HBM per device.

v0:
```python
import jax
import jax.numpy as jnp
from jax import lax
from jax.sharding import PartitionSpec as P

PAGE = 64


def turn_pairs(vectors, angle):
    half = vectors.shape[-1] // 2
    cosine, sine = (jnp.cos(angle)[None, :, None, :], jnp.sin(angle)[None, :, None, :])
    first, second = (vectors[..., :half], vectors[..., half:])
    return jnp.concatenate(
        [first * cosine - second * sine, second * cosine + first * sine], axis=-1
    )


def prepare_keys(plain_keys, angle):
    wide_keys = plain_keys.astype(jnp.float32)
    return turn_pairs(wide_keys, angle)


def per_device(raw_keys, raw_values, turn_angle):
    my_angles = lax.dynamic_slice_in_dim(
        turn_angle, lax.axis_index(("outer", "inner")) * raw_keys.shape[1], raw_keys.shape[1]
    )
    sent_keys = prepare_keys(raw_keys, my_angles).astype(jnp.bfloat16)
    moved_keys, stored_values = (
        lax.all_to_all(sent_keys, ("outer", "inner"), split_axis=0, concat_axis=1, tiled=True),
        lax.all_to_all(raw_values, ("outer", "inner"), split_axis=0, concat_axis=1, tiled=True),
    )
    page_view = moved_keys.reshape(
        moved_keys.shape[0], -1, PAGE, moved_keys.shape[2], moved_keys.shape[3]
    )
    page_high = jnp.max(page_view, axis=2)
    page_low = jnp.min(page_view, axis=2)
    return (moved_keys, stored_values, page_high, page_low)


def solution(mesh):
    in_specs = (
        P(None, ("outer", "inner"), "heads", None),
        P(None, ("outer", "inner"), "heads", None),
        P(),
    )
    out_specs = (
        P(("outer", "inner"), None, "heads", None),
        P(("outer", "inner"), None, "heads", None),
        P(("outer", "inner"), None, "heads", None),
        P(("outer", "inner"), None, "heads", None),
    )
    return jax.shard_map(
        per_device, mesh=mesh, in_specs=in_specs, out_specs=out_specs, check_vma=False
    )
```

profile of v0, /device:TPU:0, one launch (start us, length us, event | category | flops | bytes accessed | tf_op | source)
XLA Modules:
  0.0 85.2 jit_solution(4027440971430621095)
XLA Ops:
  0.6 1.4 %dynamic-slice_cosine_fusion = (f32[512,64]{0,1:T(8,128)S(1)}, f32[512,64]{0,1:T(8,128)S(1)}) fusion(f32[4096,64]{0,1:T(8,128)} %param.5, s32[]{:T(128)S(6)} %select_n.3), kind=kLoop, calls=%fused_computation.4 | loop fusion | bytes 393220 | tf_op jit(solution)/shard_map/cos | solution.py:11
  2.0 0.1 copy.7
  2.1 0.1 copy.8
  2.3 3.0 %convert_element_type.4 = f32[8,512,2,128]{3,2,1,0:T(2,128)S(1)} convert(bf16[8,512,2,128]{3,2,1,0:T(2,128)(2,1)} %param.3) | non-fusion elementwise | flops 1048576 | bytes 6291456 | tf_op jit(solution)/shard_map/convert_element_type | solution.py:19
  5.3 5.8 %subtract_convert_fusion = (bf16[8,512,2,64]{3,2,1,0:T(2,128)(2,1)S(1)}, bf16[8,512,2,64]{3,2,1,0:T(2,128)(2,1)S(1)}) fusion(f32[8,512,2,128]{3,2,1,0:T(2,128)S(1)} %convert_element_type.4, f32[512,64]{1,0:T(8,128)S(1)} %copy.8, f32[512,64]{1,0:T(8,128)S(1)} %copy.7), kind=kLoop, calls=%fused_computation.1 | loop fusion | flops 4194304 | bytes 6553600 | tf_op jit(solution)/shard_map/convert
  11.1 5.8 %pad_maximum_fusion = bf16[8,512,2,128]{3,2,1,0:T(2,128)(2,1)S(1)} fusion(bf16[8,512,2,64]{3,2,1,0:T(2,128)(2,1)S(1)} %get-tuple-element.7, bf16[8,512,2,64]{3,2,1,0:T(2,128)(2,1)S(1)} %get-tuple-element.6), kind=kLoop, calls=%fused_computation.2 | loop fusion | flops 4194304 | bytes 4194304 | tf_op jit(solution)/shard_map/concatenate | solution.py:13
  16.9 31.6 %all_to_all.24 = bf16[8,512,2,128]{3,2,1,0:T(2,128)(2,1)S(1)} all-to-all(bf16[8,512,2,128]{3,2,1,0:T(2,128)(2,1)S(1)} %pad_maximum_fusion), channel_id=1, replica_groups=mesh['outer'=2,'inner'=4,'heads'=4] {'outer','inner'}, dimensions={0} | all-to-all | bytes 4194304 | tf_op jit(solution)/shard_map/all_to_all | solution.py:29
  48.4 4.3 %all-to-all-start.1 = ((bf16[8,512,2,128]{3,2,1,0:T(2,128)(2,1)}), bf16[8,512,2,128]{3,2,1,0:T(2,128)(2,1)}, u32[]{:S(2)}, u32[]{:S(2)}) async-start(bf16[8,512,2,128]{3,2,1,0:T(2,128)(2,1)} %param.4), calls=%async_computation.1 | async-start | bytes 4194304 | tf_op jit(solution)/shard_map/all_to_all | solution.py:30
  52.8 6.5 %fusion = (bf16[64,2,128]{2,1,0:T(2,128)(2,1)}, bf16[64,2,128]{2,1,0:T(2,128)(2,1)}) fusion(bf16[1,64,64,2,128]{4,3,2,1,0:T(2,128)(2,1)S(1)} %bitcast.5), kind=kLoop, calls=%fused_computation.5 | loop fusion | flops 2064384 | bytes 2162688 | tf_op jit(solution)/shard_map/reduce_min | solution.py:36
  59.3 20.1 %all-to-all-done.1 = bf16[8,512,2,128]{3,2,1,0:T(2,128)(2,1)} async-done(((bf16[8,512,2,128]{3,2,1,0:T(2,128)(2,1)}), bf16[8,512,2,128]{3,2,1,0:T(2,128)(2,1)}, u32[]{:S(2)}, u32[]{:S(2)}) %all-to-all-start.1) | async-done | bytes 2097184 | tf_op jit(solution)/shard_map/all_to_all | solution.py:30
  79.4 1.3 %copy.11 = bf16[1,4096,2,128]{3,2,1,0:T(2,128)(2,1)} copy(bf16[1,4096,2,128]{3,2,1,0:T(2,128)(2,1)S(1)} %bitcast.6) | data formatting | bytes 4194304
  80.7 4.4 %copy.12 = bf16[1,4096,2,128]{3,2,1,0:T(2,128)(2,1)} copy(bf16[1,4096,2,128]{3,2,1,0:T(2,128)(2,1)} %bitcast.1) | data formatting | bytes 4194304
Async XLA Ops:
  48.4 31.0 %all-to-all-start.1 = ((bf16[8,512,2,128]{3,2,1,0:T(2,128)(2,1)}), bf16[8,512,2,128]{3,2,1,0:T(2,128)(2,1)}, u32[]{:S(2)}, u32[]{:S(2)}) async-start(bf16[8,512,2,128]{3,2,1,0:T(2,128)(2,1)} %param.4), calls=%async_computation.1 | async-start | bytes 4194304 | tf_op jit(solution)/shard_map/all_to_all | solution.py:30
where the time goes:
time: 85.5 us; the launch traced here: 85.2 us
  blocking collectives  31.6 us (37%)
  other arithmetic  21.1 us (25%)
  waiting for transfers between devices  20.1 us (24%)
  local copies, waits for them, and re-layouts  7.37 us (9%)
  starting transfers between devices  4.34 us (5%)
    all_to_all x1, blocking collectives, per_device(): lax.all_to_all(sent_keys, ('outer', 'inner'), split_axis=0, concat_axis=1...  31.6 us
    all_to_all x1, waiting for transfers between devices, per_device(): lax.all_to_all(raw_values, ('outer', 'inner'), split_axis=0, concat_axis=...  20.1 us
    reduce_min x1, other arithmetic, per_device(): page_low = jnp.min(page_view, axis=2)  6.5 us
    another operation x1, other arithmetic  5.78 us
    concatenate x1, other arithmetic, turn_pairs(): jnp.concatenate([first * cosine - second * sine, second * cosine + first...  5.76 us
    unnamed x2, local copies, waits for them, and re-layouts  5.75 us
    all_to_all x1, starting transfers between devices, per_device(): lax.all_to_all(raw_values, ('outer', 'inner'), split_axis=0, concat_axis=...  4.34 us
    convert_element_type x1, other arithmetic, prepare_keys(): wide_keys = plain_keys.astype(jnp.float32)  3.04 us
  transfers between devices with their start and end apart: 1, of which 1 were waited for; matrix products, arithmetic and copies ran while one was open for 8% of the time, Pallas kernels for 0%

commit v1 on v0

v1 whole, which is shorter than its diff:
```python
import functools

import jax
import jax.numpy as jnp
from jax import lax
from jax.experimental import pallas as pl
from jax.experimental.pallas import tpu as pltpu
from jax.sharding import PartitionSpec as P

PAGE = 64
MESH = pl.DeviceIdType.MESH


def offsets(outer, inner):
    cores = 2 if inner % 2 == 0 else 1
    chips = inner // cores
    steps = [
        (do, dx, dc)
        for dc in range(cores)
        for do in range(outer)
        for dx in range(chips)
        if (do, dx, dc) != (0, 0, 0)
    ]
    return cores, chips, sorted(steps, key=lambda s: (s[0] != 0) + (s[1] != 0))


def kernel(
    outer, inner, heads,
    keys, values, angle,
    out_keys, out_values, out_high, out_low,
    landed, angles, table, wide, turned, bound,
    send_k, recv_k, send_v, recv_v, local,
):
    group = outer * inner
    batch, rows, size = keys.shape
    own = batch // group
    length = rows // heads
    half = size // 2
    pages = length // PAGE
    cores, chips, steps = offsets(outer, inner)
    o, i = lax.axis_index("outer"), lax.axis_index("inner")
    x, c = i // cores, i % cores
    me = o * inner + i

    def partner(step, sign):
        do, dx, dc = step
        po = (o + sign * do + outer) % outer
        pi = (x + sign * dx + chips) % chips * cores + (c + sign * dc + cores) % cores
        return po, pi

    get_angles = pltpu.make_async_copy(angle, angles, local.at[0])
    get_angles.start()
    mine = pl.ds(pl.multiple_of(me * rows, rows), rows)
    own_keys = pltpu.make_async_copy(
        keys.at[pl.ds(me * own, own)], landed.at[:, mine], local.at[1]
    )
    own_values = pltpu.make_async_copy(
        values.at[pl.ds(me * own, own)], out_values.at[:, mine], local.at[2]
    )
    own_keys.start()
    own_values.start()

    barrier = pltpu.get_barrier_semaphore()
    for step in steps:
        po, pi = partner(step, 1)
        pl.semaphore_signal(
            barrier, inc=1, device_id={"outer": po, "inner": pi}, device_id_type=MESH
        )
    pl.semaphore_wait(barrier, len(steps))

    copies_k, copies_v = [], []
    for j, step in enumerate(steps):
        po, pi = partner(step, 1)
        theirs = pl.ds((po * inner + pi) * own, own)
        for copies, src, dst, send, recv in (
            (copies_k, keys, landed, send_k, recv_k),
            (copies_v, values, out_values, send_v, recv_v),
        ):
            copies.append(
                pltpu.make_async_remote_copy(
                    src_ref=src.at[theirs],
                    dst_ref=dst.at[:, mine],
                    send_sem=send.at[j],
                    recv_sem=recv.at[j],
                    device_id={"outer": po, "inner": pi},
                    device_id_type=MESH,
                )
            )
    far = [(s[0] != 0) + (s[1] != 0) for s in steps]
    for distance in sorted(set(far)):
        for copies in (copies_k, copies_v):
            for j, copy in enumerate(copies):
                if far[j] == distance:
                    copy.start()

    get_angles.wait()

    def fill(p, carry):
        at = pl.ds(pl.multiple_of(p * size, size), size)
        a = angles[:, at]
        table[at] = jnp.concatenate([jnp.cos(a), jnp.sin(a)], axis=0).T
        return carry

    lax.fori_loop(0, table.shape[0] // size, fill, 0)

    def turn(source):
        for n in range(own):
            def page(p, carry):
                at = pl.multiple_of(source * length + p * PAGE, PAGE)
                tab = table[pl.ds(at, PAGE)]
                swap = pltpu.roll(tab, half, 1)
                low_half = lax.broadcasted_iota(jnp.int32, tab.shape, 1) < half
                cosine = jnp.where(low_half, tab, swap)
                sine = jnp.where(low_half, -swap, tab)
                at_rows = pl.ds(pl.multiple_of(at * heads, PAGE * heads), PAGE * heads)
                wide[...] = landed[n, at_rows].astype(jnp.float32)
                for h in range(heads):
                    v = wide[pl.ds(h, PAGE, stride=heads)]
                    y = v * cosine + pltpu.roll(v, half, 1) * sine
                    turned[pl.ds(h, PAGE, stride=heads)] = y
                    bound[0, pl.ds(p * heads + h, 1)] = jnp.max(y, axis=0, keepdims=True)
                    bound[1, pl.ds(p * heads + h, 1)] = jnp.min(y, axis=0, keepdims=True)
                out_keys[n, at_rows] = turned[...].astype(out_keys.dtype)
                return carry

            lax.fori_loop(0, pages, page, 0)
            at_pages = pl.ds(pl.multiple_of(source * pages * heads, pages * heads), pages * heads)
            out_high[n, at_pages] = bound[0].astype(out_high.dtype)
            out_low[n, at_pages] = bound[1].astype(out_low.dtype)

    own_keys.wait()
    turn(me)
    for j, step in enumerate(steps):
        copies_k[j].wait_recv()
        po, pi = partner(step, -1)
        turn(po * inner + pi)
    own_values.wait()
    for j in range(len(steps)):
        copies_v[j].wait_recv()
    for j in range(len(steps)):
        copies_k[j].wait_send()
        copies_v[j].wait_send()


def per_device(outer, inner, raw_keys, raw_values, turn_angle):
    batch, length, heads, size = raw_keys.shape
    group = outer * inner
    own, rows, pages = batch // group, length * heads, length // PAGE
    bf16, f32 = jnp.bfloat16, jnp.float32
    scratch_bytes = group * length * size * (2 * own * heads + 8) + 2**22
    outs = pl.pallas_call(
        functools.partial(kernel, outer, inner, heads),
        out_shape=(
            pltpu.VMEM((own, group * rows, size), bf16),
            pltpu.VMEM((own, group * rows, size), bf16),
            pltpu.VMEM((own, group * pages * heads, size), bf16),
            pltpu.VMEM((own, group * pages * heads, size), bf16),
        ),
        in_specs=[pl.BlockSpec(memory_space=pltpu.HBM)] * 3,
        out_specs=[pl.BlockSpec(memory_space=pltpu.VMEM)] * 4,
        scratch_shapes=[
            pltpu.VMEM((own, group * rows, size), bf16),
            pltpu.VMEM((turn_angle.shape[1], turn_angle.shape[0]), f32),
            pltpu.VMEM((turn_angle.shape[0], size), f32),
            pltpu.VMEM((PAGE * heads, size), f32),
            pltpu.VMEM((PAGE * heads, size), f32),
            pltpu.VMEM((2, pages * heads, size), f32),
            pltpu.SemaphoreType.DMA((group,)),
            pltpu.SemaphoreType.DMA((group,)),
            pltpu.SemaphoreType.DMA((group,)),
            pltpu.SemaphoreType.DMA((group,)),
            pltpu.SemaphoreType.DMA((3,)),
        ],
        compiler_params=pltpu.CompilerParams(
            collective_id=0, has_side_effects=True, vmem_limit_bytes=scratch_bytes
        ),
    )(
        raw_keys.reshape(batch, rows, size),
        raw_values.reshape(batch, rows, size),
        turn_angle.T,
    )
    keys, values, high, low = outs
    return (
        keys.reshape(own, group * length, heads, size),
        values.reshape(own, group * length, heads, size),
        high.reshape(own, group * pages, heads, size),
        low.reshape(own, group * pages, heads, size),
    )


def solution(mesh):
    moved = P(None, ("outer", "inner"), "heads", None)
    whole = P(("outer", "inner"), None, "heads", None)
    return jax.shard_map(
        functools.partial(per_device, mesh.shape["outer"], mesh.shape["inner"]),
        mesh=mesh,
        in_specs=(moved, moved, P()),
        out_specs=(whole,) * 4,
        check_vma=False,
    )
```

time: 85.5 us -> 59.5 us (0.70)
  Pallas kernels: 0 us -> 50.3 us
  blocking collectives: 31.6 us -> 0 us
  other arithmetic: 21.1 us -> 0 us
  waiting for transfers between devices: 20.1 us -> 0 us
  starting transfers between devices: 4.34 us -> 0 us
  local copies, waits for them, and re-layouts: 7.37 us -> 8.27 us
    pallas_call x0 -> x1, Pallas kernels: none -> 50.3 us  [per_device(): pl.pallas_call(functools.partial(kernel, outer, inner, heads), out_shape=...]
    all_to_all x1 -> x0, blocking collectives: 31.6 us -> none  [per_device(): lax.all_to_all(sent_keys, ('outer', 'inner'), split_axis=0, concat_axis=1...]
    all_to_all x1 -> x0, waiting for transfers between devices: 20.1 us -> none  [per_device(): lax.all_to_all(raw_values, ('outer', 'inner'), split_axis=0, concat_axis=...]
    reduce_min x1 -> x0, other arithmetic: 6.5 us -> none  [per_device(): page_low = jnp.min(page_view, axis=2)]
    another operation x1 -> x0, other arithmetic: 5.78 us -> none
    concatenate x1 -> x0, other arithmetic: 5.76 us -> none  [turn_pairs(): jnp.concatenate([first * cosine - second * sine, second * cosine + first...]
    all_to_all x1 -> x0, starting transfers between devices: 4.34 us -> none  [per_device(): lax.all_to_all(raw_values, ('outer', 'inner'), split_axis=0, concat_axis=...]
    convert_element_type x1 -> x0, other arithmetic: 3.04 us -> none  [prepare_keys(): wide_keys = plain_keys.astype(jnp.float32)]
  transfers between devices with their start and end apart: 1 -> 0, of which waited for: 1 -> 0; matrix products, arithmetic and copies ran while one was open for 8% -> 0% of each run, Pallas kernels for 0% -> 0%
where the time goes in v1:
time: 59.5 us; the launch traced here: 59.2 us
  Pallas kernels  50.3 us (85%)
  local copies, waits for them, and re-layouts  8.27 us (14%)
  between operations  0.65 us (1%)
    pallas_call x1, Pallas kernels, per_device(): pl.pallas_call(functools.partial(kernel, outer, inner, heads), out_shape=...  50.3 us
    unnamed x10, local copies, waits for them, and re-layouts  8.27 us

profile of v1, /device:TPU:0, one launch (start us, length us, event | category | flops | bytes accessed | tf_op | source)
XLA Modules:
  0.0 59.2 jit_solution(5163883381578406032)
XLA Ops:
  0.6 0.0 copy-start
  0.6 1.6 %copy-done = bf16[8,512,2,128]{3,2,1,0:T(2,128)(2,1)S(1)} copy-done((bf16[8,512,2,128]{3,2,1,0:T(2,128)(2,1)S(1)}, bf16[8,512,2,128]{3,2,1,0:T(2,128)(2,1)}, u32[]{:S(2)}) %copy-start) | copy-done | bytes 2097176
  2.2 0.0 copy-start.1
  2.2 1.6 %copy-done.1 = bf16[8,512,2,128]{3,2,1,0:T(2,128)(2,1)S(1)} copy-done((bf16[8,512,2,128]{3,2,1,0:T(2,128)(2,1)S(1)}, bf16[8,512,2,128]{3,2,1,0:T(2,128)(2,1)}, u32[]{:S(2)}) %copy-start.1) | copy-done | bytes 2097176
  3.8 0.0 copy-start.2
  3.8 1.2 %copy-done.2 = f32[4096,64]{0,1:T(8,128)S(1)} copy-done((f32[4096,64]{0,1:T(8,128)S(1)}, f32[4096,64]{0,1:T(8,128)}, u32[]{:S(2)}) %copy-start.2) | copy-done | bytes 1048600
  5.0 50.3 %shard_map.66 = (bf16[1,8192,128]{2,1,0:T(8,128)(2,1)S(1)}, bf16[1,8192,128]{2,1,0:T(8,128)(2,1)S(1)}, bf16[1,128,128]{2,1,0:T(8,128)(2,1)S(1)}, bf16[1,128,128]{2,1,0:T(8,128)(2,1)S(1)}) custom-call(bf16[8,1024,128]{2,1,0:T(8,128)(2,1)S(1)} %bitcast.11, bf16[8,1024,128]{2,1,0:T(8,128)(2,1)S(1)} %bitcast.12, f32[64,4096]{1,0:T(8,128)S(1)} %bitcast.13), custom_call_target="tpu_custom_call" | custom-call | tf_op jit(solution)/shard_map/pallas_call | solution.py:151
  55.4 1.3 %copy.11 = bf16[1,4096,2,128]{3,2,1,0:T(2,128)(2,1)} copy(bf16[1,4096,2,128]{3,2,1,0:T(2,128)(2,1)S(1)} %bitcast.8) | data formatting | bytes 4194304
  56.7 1.3 %copy.12 = bf16[1,4096,2,128]{3,2,1,0:T(2,128)(2,1)} copy(bf16[1,4096,2,128]{3,2,1,0:T(2,128)(2,1)S(1)} %bitcast.7) | data formatting | bytes 4194304
  58.0 0.6 %copy.13 = bf16[1,64,2,128]{3,2,1,0:T(2,128)(2,1)} copy(bf16[1,64,2,128]{3,2,1,0:T(2,128)(2,1)S(1)} %bitcast.10) | data formatting | bytes 65536
  58.6 0.6 %copy.14 = bf16[1,64,2,128]{3,2,1,0:T(2,128)(2,1)} copy(bf16[1,64,2,128]{3,2,1,0:T(2,128)(2,1)S(1)} %bitcast.9) | data formatting | bytes 65536
Async XLA Ops:
  0.6 1.6 %copy-start = (bf16[8,512,2,128]{3,2,1,0:T(2,128)(2,1)S(1)}, bf16[8,512,2,128]{3,2,1,0:T(2,128)(2,1)}, u32[]{:S(2)}) copy-start(bf16[8,512,2,128]{3,2,1,0:T(2,128)(2,1)} %param.3) | copy-start | bytes 6291460
  2.2 1.6 %copy-start.1 = (bf16[8,512,2,128]{3,2,1,0:T(2,128)(2,1)S(1)}, bf16[8,512,2,128]{3,2,1,0:T(2,128)(2,1)}, u32[]{:S(2)}) copy-start(bf16[8,512,2,128]{3,2,1,0:T(2,128)(2,1)} %param.4) | copy-start | bytes 6291460
  3.8 1.2 %copy-start.2 = (f32[4096,64]{0,1:T(8,128)S(1)}, f32[4096,64]{0,1:T(8,128)}, u32[]{:S(2)}) copy-start(f32[4096,64]{0,1:T(8,128)} %param.5) | copy-start | bytes 3145732

commit v2 on v1

--- a/solution.py
+++ b/solution.py
@@ -142,6 +142,22 @@
         copies_v[j].wait_send()
 
 
+def in_hbm(array):
+    return pltpu.with_memory_space_constraint(array, pltpu.HBM)
+
+
+def store(*refs):
+    count = len(refs) // 2
+    sems = refs[-1]
+    copies = [
+        pltpu.make_async_copy(refs[k], refs[count + k], sems.at[k]) for k in range(count)
+    ]
+    for copy in copies:
+        copy.start()
+    for copy in copies:
+        copy.wait()
+
+
 def per_device(outer, inner, raw_keys, raw_values, turn_angle):
     batch, length, heads, size = raw_keys.shape
     group = outer * inner
@@ -175,11 +191,18 @@
             collective_id=0, has_side_effects=True, vmem_limit_bytes=scratch_bytes
         ),
     )(
-        raw_keys.reshape(batch, rows, size),
-        raw_values.reshape(batch, rows, size),
-        turn_angle.T,
-    )
-    keys, values, high, low = outs
+        in_hbm(raw_keys.reshape(batch, rows, size)),
+        in_hbm(raw_values.reshape(batch, rows, size)),
+        in_hbm(turn_angle.T),
+    )
+    keys, values, high, low = pl.pallas_call(
+        store,
+        out_shape=[jax.ShapeDtypeStruct(out.shape, out.dtype) for out in outs],
+        in_specs=[pl.BlockSpec(memory_space=pltpu.VMEM)] * 4,
+        out_specs=[pl.BlockSpec(memory_space=pltpu.HBM)] * 4,
+        scratch_shapes=[pltpu.SemaphoreType.DMA((4,))],
+        compiler_params=pltpu.CompilerParams(vmem_limit_bytes=2**20),
+    )(*outs)
     return (
         keys.reshape(own, group * length, heads, size),
         values.reshape(own, group * length, heads, size),

time: 59.5 us -> 53.3 us (0.90)
  local copies, waits for them, and re-layouts: 8.27 us -> 0 us
  Pallas kernels: 50.3 us -> 52.5 us
    unnamed x10 -> x0, local copies, waits for them, and re-layouts: 8.27 us -> none
    pallas_call x0 -> x1, Pallas kernels: none -> 2.05 us  [per_device(): pl.pallas_call(store, out_shape=[jax.ShapeDtypeStruct(out.shape, out.dtyp...]
where the time goes in v2:
time: 53.3 us; the launch traced here: 53.2 us
  Pallas kernels  52.5 us (98%)
  between operations  0.64 us (1%)
    pallas_call x1, Pallas kernels, per_device(): pl.pallas_call(functools.partial(kernel, outer, inner, heads), out_shape=...  50.5 us
    pallas_call x1, Pallas kernels, per_device(): pl.pallas_call(store, out_shape=[jax.ShapeDtypeStruct(out.shape, out.dtyp...  2.05 us

profile of v2, /device:TPU:0, one launch (start us, length us, event | category | flops | bytes accessed | tf_op | source)
XLA Modules:
  0.0 53.2 jit_solution(4901813396964455963)
XLA Ops:
  0.6 50.5 %shard_map.66 = (bf16[1,8192,128]{2,1,0:T(8,128)(2,1)S(1)}, bf16[1,8192,128]{2,1,0:T(8,128)(2,1)S(1)}, bf16[1,128,128]{2,1,0:T(8,128)(2,1)S(1)}, bf16[1,128,128]{2,1,0:T(8,128)(2,1)S(1)}) custom-call(bf16[8,1024,128]{2,1,0:T(8,128)(2,1)} %bitcast.7, bf16[8,1024,128]{2,1,0:T(8,128)(2,1)} %bitcast.8, f32[64,4096]{1,0:T(8,128)} %bitcast.9), custom_call_target="tpu_custom_call" | custom-call | tf_op jit(solution)/shard_map/pallas_call | solution.py:167
  51.1 2.1 %shard_map.67 = (bf16[1,8192,128]{2,1,0:T(8,128)(2,1)}, bf16[1,8192,128]{2,1,0:T(8,128)(2,1)}, bf16[1,128,128]{2,1,0:T(8,128)(2,1)}, bf16[1,128,128]{2,1,0:T(8,128)(2,1)}) custom-call(bf16[1,8192,128]{2,1,0:T(8,128)(2,1)S(1)} %get-tuple-element.12.refs_0_, bf16[1,8192,128]{2,1,0:T(8,128)(2,1)S(1)} %get-tuple-element.13.refs_1_, ...), custom_call_target="tpu_custom_call" | custom-call | tf_op jit(solution)/shard_map/pallas_call | solution.py:198
